TPU v7x, 32 devices: a whole 2x2x4 slice. The times are simulated.
32 devices in a mesh: dp: 16 (over z, y, x), mp: 2 (over core).
Axes of the slice: x: 2, y: 2, z: 4, core: 2. Of those that a mesh axis runs over, the one named last changes fastest.
Arguments:
- hidden: bfloat16 [4096, 8192], P('dp', 'mp'), may hold values from -6 to 6
- w_key: bfloat16 [8192, 1024], P('mp', 'dp'), may hold values from -0.0625 to 0.0625
- w_value: bfloat16 [8192, 1024], P('mp', 'dp'), may hold values from -0.0625 to 0.0625
- queries: bfloat16 [4096, 8192], P('dp', 'mp'), may hold values from -150 to 150
- lengths: int32 [16], replicated, may hold values from 1 to 512, as said below
- seq_of_slot: int32 [32], replicated, may hold values from 0 to 15, as said below
- pos_of_slot: int32 [32], replicated, may hold values from 0 to 3, as said below
Outputs:
- context: bfloat16 [4096, 8192], P('dp', 'mp')
- key_cache: bfloat16 [16, 512, 1024], P('dp', None, 'mp')
- value_cache: bfloat16 [16, 512, 1024], P('dp', None, 'mp')
Inputs may be any that keep to these rules, and one draw needn't show every extreme that they name: Sequence q has ceil(lengths[q] / 128) blocks, 1 to 4; some sequence has 4 full blocks. `seq_of_slot`: slots 2 i and 2 i + 1 belong to replica i. Every block of every sequence stands in exactly one slot. The blocks of one sequence stand on different replicas; the two slots of a replica hold blocks of different sequences; and for any two replicas A and B, at most one block on A is an earlier block of the same sequence as some block on B. `pos_of_slot`: given with seq_of_slot: the block index, from 0, of the block in each slot.
All inputs are finite; a program needn't handle non-finite values.
Results may differ from a plain program's by a relative error of at most 0.011.
Values may be sent and summed in bfloat16 or wider, within the bound.
A program may use at most 128 MiB of HBM per device.

v0:
```python
import math

import jax
import jax.numpy as jnp
from jax import lax
from jax.sharding import PartitionSpec as P

HQ = 64
KVH = 8
HD = 128
BLOCK = 128
MAXB = 4


def rotate(field, positions):
    halfway = field.shape[-1] // 2
    indices = jnp.arange(halfway, dtype=jnp.float32)
    frequency = jnp.exp(-(2.0 * indices / field.shape[-1]) * math.log(500000.0))
    angles = positions[:, None] * frequency[None, :]
    cosines = jnp.cos(angles)[:, None, :]
    sines = jnp.sin(angles)[:, None, :]
    front = field[..., :halfway]
    back = field[..., halfway:]
    return jnp.concatenate(
        [front * cosines - back * sines, back * cosines + front * sines], axis=-1
    )


def shards(hidden, w_key, w_value, queries, lengths, seq_of_slot, pos_of_slot):
    replica = lax.axis_index("dp")
    token_rows = hidden.shape[0]
    local_slots = token_rows // BLOCK
    key_full, value_full = (
        lax.all_gather(w_key, "dp", axis=1, tiled=True),
        lax.all_gather(w_value, "dp", axis=1, tiled=True),
    )
    key_sum = jnp.dot(hidden, key_full, preferred_element_type=jnp.float32)
    value_sum = jnp.dot(hidden, value_full, preferred_element_type=jnp.float32)
    key_raw, value_raw = (
        lax.psum_scatter(key_sum, "mp", scatter_dimension=1, tiled=True),
        lax.psum_scatter(value_sum, "mp", scatter_dimension=1, tiled=True),
    )
    head_width = key_raw.shape[1]
    local_heads = head_width // HD
    my_seq = lax.dynamic_slice_in_dim(seq_of_slot, replica * local_slots, local_slots)
    my_pos = lax.dynamic_slice_in_dim(pos_of_slot, replica * local_slots, local_slots)
    offsets = jnp.arange(BLOCK, dtype=jnp.int32)
    query_pos = my_pos[:, None] * BLOCK + offsets[None, :]
    key_rows = rotate(
        key_raw.reshape(token_rows, local_heads, HD),
        query_pos.reshape(token_rows).astype(jnp.float32),
    )
    key_rows = key_rows.reshape(token_rows, head_width).astype(jnp.bfloat16)
    value_rows = value_raw.astype(jnp.bfloat16)
    payload = jnp.concatenate([key_rows, value_rows], axis=1).reshape(
        local_slots, BLOCK * 2 * head_width
    )
    blocks = jnp.arange(MAXB, dtype=jnp.int32)
    needed = (
        (seq_of_slot[None, None, :] == my_seq[:, None, None])
        & (pos_of_slot[None, None, :] == blocks[None, :, None])
        & (blocks[None, :, None] < my_pos[:, None, None])
    )
    owned = (seq_of_slot[None, :] == replica) & (pos_of_slot[None, :] == blocks[:, None])
    needed_pick = needed.astype(jnp.bfloat16)
    owned_pick = owned.astype(jnp.bfloat16)
    portion = lax.all_gather(payload, "dp", axis=0, tiled=True)
    earlier = jnp.einsum("smn,nx->smx", needed_pick, portion, preferred_element_type=jnp.float32)
    home_rows = jnp.dot(owned_pick, portion, preferred_element_type=jnp.float32)
    own_block = (blocks[None, :] == my_pos[:, None]).astype(jnp.float32)
    assembled = (earlier + own_block[:, :, None] * payload[:, None, :].astype(jnp.float32)).astype(
        jnp.bfloat16
    )
    span = MAXB * BLOCK
    assembled = assembled.reshape(local_slots, span, 2 * head_width)
    key_blocks = assembled[:, :, :head_width].reshape(local_slots, span, local_heads, HD)
    value_blocks = assembled[:, :, head_width:].reshape(local_slots, span, local_heads, HD)
    ratio = HQ // KVH
    query_blocks = queries.reshape(local_slots, BLOCK, local_heads, ratio, HD)
    scores = jnp.einsum(
        "sbgrd,scgd->sgrbc", query_blocks, key_blocks, preferred_element_type=jnp.float32
    ) * (1.0 / math.sqrt(HD))
    slot_lengths = lengths[my_seq]
    cached = jnp.arange(span, dtype=jnp.int32)
    allowed = (cached[None, None, :] <= query_pos[:, :, None]) & (
        cached[None, None, :] < slot_lengths[:, None, None]
    )
    scores = jnp.where(allowed[:, None, None], scores, -1e30)
    largest = jnp.max(scores, axis=-1, keepdims=True)
    weights = jnp.exp(scores - largest)
    probs = (weights / jnp.sum(weights, axis=-1, keepdims=True)).astype(jnp.bfloat16)
    mixed = jnp.einsum("sgrbc,scgd->sbgrd", probs, value_blocks, preferred_element_type=jnp.float32)
    valid = query_pos < slot_lengths[:, None]
    mixed = jnp.where(valid[:, :, None, None, None], mixed, 0.0)
    context = mixed.reshape(token_rows, local_heads * ratio * HD).astype(jnp.bfloat16)
    cache_rows = home_rows.reshape(span, 2 * head_width)
    own_length = lax.dynamic_slice_in_dim(lengths, replica, 1)[0]
    cache_rows = jnp.where((cached < own_length)[:, None], cache_rows, 0.0).astype(jnp.bfloat16)
    return (context, cache_rows[None, :, :head_width], cache_rows[None, :, head_width:])


def solution(mesh):
    in_specs = (P("dp", "mp"), P("mp", "dp"), P("mp", "dp"), P("dp", "mp"), P(), P(), P())
    out_specs = (P("dp", "mp"), P("dp", None, "mp"), P("dp", None, "mp"))
    return jax.shard_map(shards, mesh=mesh, in_specs=in_specs, out_specs=out_specs, check_vma=False)
```

profile of v0, /device:TPU:0, one launch (start us, length us, event | category | flops | bytes accessed | tf_op | source)
XLA Modules:
  0.0 450.9 jit_solution(2010580161940887046)
XLA Ops:
  7.2 0.7 all-gather.5.cloned.1.call-update
  8.0 0.7 all-gather.7.cloned.1.call-update
  8.7 117.1 %all-gather.5.cloned.1.call-done = bf16[4096,1024]{0,1:T(8,128)(2,1)} async-done(((bf16[4096,64]{0,1:T(8,128)(2,1)}), bf16[4096,1024]{0,1:T(8,128)(2,1)}) %all-gather.5.cloned.1.call-update) | async-done | bytes 8388624 | tf_op jit(solution)/shard_map/all_gather | solution.py:34
  125.8 6.7 %fusion.36 = f32[256,1024]{1,0:T(8,128)} fusion(bf16[256,4096]{1,0:T(8,128)(2,1)S(1)} %copy-done, bf16[4096,1024]{0,1:T(8,128)(2,1)} %all-gather.5.cloned.1.call-done), kind=kOutput, calls=%fused_computation.57 | convolution fusion | flops 2147483648 | bytes 11534336 | tf_op jit(solution)/shard_map/dot_general | solution.py:37
  132.6 106.4 %all-gather.7.cloned.1.call-done = bf16[4096,1024]{0,1:T(8,128)(2,1)} async-done(((bf16[4096,64]{0,1:T(8,128)(2,1)}), bf16[4096,1024]{0,1:T(8,128)(2,1)}) %all-gather.7.cloned.1.call-update) | async-done | bytes 8388624 | tf_op jit(solution)/shard_map/all_gather | solution.py:35
  239.1 6.7 %fusion.37 = f32[256,1024]{1,0:T(8,128)} fusion(bf16[256,4096]{1,0:T(8,128)(2,1)S(1)} %copy-done, bf16[4096,1024]{0,1:T(8,128)(2,1)} %all-gather.7.cloned.1.call-done), kind=kOutput, calls=%fused_computation.58 | convolution fusion | flops 2147483648 | bytes 11534336 | tf_op jit(solution)/shard_map/dot_general | solution.py:38
  246.6 1.3 reduce-scatter.3.cloned.1.call-done
  247.9 1.2 reshape.292
  250.1 10.1 %reduce-scatter.5.cloned.1.call-done = f32[256,512]{1,0:T(8,128)} async-done(((f32[256,1024]{1,0:T(8,128)}), f32[256,512]{1,0:T(8,128)}) %reduce-scatter.5.cloned.1.call-update) | async-done | bytes 524304 | tf_op jit(solution)/shard_map/reduce_scatter | solution.py:41
  260.2 1.1 convert_element_type.55
  261.4 1.2 reshape.308
  262.6 0.6 dynamic_slice.11
  263.2 0.6 gather_fusion
  263.9 3.4 copy.32
  267.3 0.6 iota_compare_fusion.2
  268.5 0.9 reshape.311
  269.4 107.5 %all-gather.9.cloned.1.call-done = bf16[16,2,131072]{2,1,0:T(2,128)(2,1)} async-done(((bf16[1,2,131072]{2,1,0:T(2,128)(2,1)}), bf16[16,2,131072]{2,1,0:T(2,128)(2,1)}) %all-gather.9.cloned.1.call-update) | async-done | bytes 8388624 | tf_op jit(solution)/shard_map/all_gather | solution.py:67
  376.9 8.4 %reshape.312 = bf16[32,131072,1]{1,0,2:T(8,128)(2,1)} reshape(bf16[16,2,131072]{2,1,0:T(2,128)(2,1)} %all-gather.9.cloned.1.call-done) | data formatting | bytes 16777216
  385.3 6.6 %fusion.1 = bf16[2,4,131072]{2,1,0:T(4,128)(2,1)} fusion(bf16[32,131072,1]{1,0,2:T(8,128)(2,1)} %reshape.312, f32[2,131072]{1,0:T(2,128)S(1)} %reshape.311, f32[2,4]{1,0:T(2,128)S(1)} %get-tuple-element.20, pred[2,4]{1,0:T(4,128)(4,1)S(1)} %get-tuple-element.19, pred[4,32]{1,0:T(4,128)(4,1)S(1)} %iota_compare_fusion.3, ...), kind=kOutput, calls=%fused_computation.3 | convolution fusion | flops 70255104 | bytes 11534568 | tf_op jit(solution)/shard_map/smn,nx->smx/dot_general | solution.py:68
  391.9 3.1 reshape.294
  394.9 8.4 %reshape.309 = bf16[32,131072]{1,0:T(8,128)(2,1)} reshape(bf16[16,2,131072]{2,1,0:T(2,128)(2,1)} %all-gather.9.cloned.1.call-done) | data formatting | bytes 16777216
  403.3 4.6 %fusion.20 = bf16[4,131072]{1,0:T(4,128)(2,1)S(1)} fusion(bf16[32,131072]{1,0:T(8,128)(2,1)} %reshape.309, pred[32]{0:T(512)(128)(4,1)S(1)} %broadcast_compare_fusion.1, s32[32]{0:T(128)S(1)} %copy-done.4), kind=kOutput, calls=%fused_computation.37 | convolution fusion | flops 33554688 | bytes 9437344 | tf_op jit(solution)/shard_map/dot_general | solution.py:69
  407.9 1.9 reshape.298
  409.8 1.5 select_convert_fusion.1
  411.3 1.0 slice_bitcast_fusion
  412.3 1.2 fusion.30
  413.5 1.5 copy.30
  415.0 1.3 copy.19
  416.3 10.7 %fusion.31 = (f32[2,4,8,128]{3,2,1,0:T(8,128)S(1)}, f32[2,4,8,128,512]{3,4,2,1,0:T(8,128)}) fusion(bf16[2,512,4,128,1]{1,3,4,2,0:T(8,128)(2,1)S(1)} %bitcast.52, pred[2,128,512]{1,2,0:T(8,128)(4,1)S(1)} %fusion.17, bf16[2,128,4,8,128]{4,3,2,1,0:T(8,128)(2,1)} %bitcast.49), kind=kOutput, calls=%fused_computation.56 | convolution fusion | flops 1090519552 | bytes 20086784 | tf_op jit(solution)/shard_map/sub | solution.py:90
  427.0 8.7 %fusion.9 = bf16[2,128,4,8,128]{1,4,3,2,0:T(8,128)(2,1)} fusion(pred[2,128]{1,0:T(4,128)(4,1)S(1)} %fusion.26, bf16[2,512,4,128,1]{1,3,4,2,0:T(8,128)(2,1)S(1)} %bitcast.51, f32[2,4,8,128,512]{3,4,2,1,0:T(8,128)} %get-tuple-element.22, f32[2,4,8,128]{3,2,1,0:T(8,128)S(1)} %get-tuple-element.21), kind=kOutput, calls=%fused_computation.14 | convolution fusion | flops 1084227584 | bytes 19955968 | tf_op jit(solution)/shard_map/sgrbc,scgd->sbgrd/dot_general | solution.py:92
  435.7 4.6 %copy.24 = bf16[2,128,4,8,128]{4,3,2,1,0:T(8,128)(2,1)} copy(bf16[2,128,4,8,128]{1,4,3,2,0:T(8,128)(2,1)} %fusion.9) | data formatting | bytes 4194304 | tf_op jit(solution)/shard_map/convert_element_type | solution.py:95
  440.2 4.2 convert_element_type.62
  (36 shorter events, 2.6 us)
Async XLA Ops:
  7.2 118.7 %copy-start = (bf16[256,4096]{1,0:T(8,128)(2,1)S(1)}, bf16[256,4096]{1,0:T(8,128)(2,1)}, u32[]{:S(2)}) copy-start(bf16[256,4096]{1,0:T(8,128)(2,1)} %param.7) | copy-start | bytes 6291460
  7.2 118.6 %all-gather.5.cloned.1.call-start = ((), (), s32[]{:S(2)}) async-start(), calls=%async_computation.2 | async-start | bytes 8912896 | tf_op jit(solution)/shard_map/all_gather | solution.py:34
  7.9 231.2 %all-gather.7.cloned.1.call-start = ((), (), s32[]{:S(2)}) async-start(), calls=%async_computation.4 | async-start | bytes 8912896 | tf_op jit(solution)/shard_map/all_gather | solution.py:35
  8.7 239.3 %reduce-scatter.3.cloned.1.call-start = ((), (), s32[]{:S(2)}) async-start(), calls=%async_computation.3 | async-start | bytes 1572864 | tf_op jit(solution)/shard_map/reduce_scatter | solution.py:40
  132.6 113.3 %copy-start.4 = (s32[32]{0:T(128)S(1)}, s32[32]{0:T(128)}, u32[]{:S(2)}) copy-start(s32[32]{0:T(128)} %param.13) | copy-start | bytes 388
  132.6 113.3 %copy-start.5 = (s32[32]{0:T(128)S(1)}, s32[32]{0:T(128)}, u32[]{:S(2)}) copy-start(s32[32]{0:T(128)} %param.12) | copy-start | bytes 388
  132.6 127.6 %reduce-scatter.5.cloned.1.call-start = ((), (), s32[]{:S(2)}) async-start(), calls=%async_computation.5 | async-start | bytes 1572864 | tf_op jit(solution)/shard_map/reduce_scatter | solution.py:41
  245.8 16.8 %copy-start.2 = (s32[16]{0:T(128)S(1)}, s32[16]{0:T(128)}, u32[]{:S(2)}) copy-start(s32[16]{0:T(128)} %param.11) | copy-start | bytes 196
  245.8 131.0 %all-gather.9.cloned.1.call-start = ((), (), s32[]{:S(2)}) async-start(), calls=%async_computation.6 | async-start | bytes 8912896 | tf_op jit(solution)/shard_map/all_gather | solution.py:67
  416.3 10.7 %copy-start.3 = (bf16[2,512,512]{1,2,0:T(8,128)(2,1)S(1)}, bf16[2,512,512]{1,2,0:T(8,128)(2,1)}, u32[]{:S(2)}) copy-start(bf16[2,512,512]{1,2,0:T(8,128)(2,1)} %copy.19) | copy-start | bytes 3145732
  427.0 17.4 %copy-start.1 = (bf16[256,4096]{1,0:T(8,128)(2,1)S(1)}, bf16[256,4096]{1,0:T(8,128)(2,1)}, u32[]{:S(2)}) copy-start(bf16[256,4096]{1,0:T(8,128)(2,1)} %param.7) | copy-start | bytes 6291460
Sparse Core Ops, SparseCore 0:
  10.8 115.0 all-gather.4
  128.6 110.4 all-gather.6
  241.3 6.5 reduce-scatter.2
  250.6 9.5 reduce-scatter.4
  263.4 113.4 all-gather.8
where the time goes:
time: 452 us; the launch traced here: 451 us
  waiting for transfers between devices  344 us (76%)
  matrix products  43.9 us (10%)
  local copies, waits for them, and re-layouts  43.5 us (10%)
  between operations  14 us (3%)
  other arithmetic  5.44 us (1%)
    all_gather x1, waiting for transfers between devices, shards(): lax.all_gather(w_key, 'dp', axis=1, tiled=True)  117 us
    all_gather x1, waiting for transfers between devices, shards(): portion = lax.all_gather(payload, 'dp', axis=0, tiled=True)  108 us
    all_gather x1, waiting for transfers between devices, shards(): lax.all_gather(w_value, 'dp', axis=1, tiled=True)  106 us
    unnamed x18, local copies, waits for them, and re-layouts  23 us
    sub x1, matrix products, shards(): weights = jnp.exp(scores - largest)  10.7 us
    reduce_scatter x1, waiting for transfers between devices, shards(): lax.psum_scatter(value_sum, 'mp', scatter_dimension=1, tiled=True)  10.1 us
  transfers between devices with their start and end apart: 5, of which 5 were waited for; matrix products, arithmetic and copies ran while one was open for 5% of the time, Pallas kernels for 0%

commit v1 on v0

--- a/solution.py
+++ b/solution.py
@@ -1,8 +1,11 @@
+import functools
 import math
 
 import jax
 import jax.numpy as jnp
 from jax import lax
+from jax.experimental import pallas as pl
+from jax.experimental.pallas import tpu as pltpu
 from jax.sharding import PartitionSpec as P
 
 HQ = 64
@@ -99,7 +102,459 @@
     return (context, cache_rows[None, :, :head_width], cache_rows[None, :, head_width:])
 
 
+MESH = pl.DeviceIdType.MESH
+PAYLOAD_ORDERS = (("z", "x", "y"), ("y", "z", "x"), ("x", "y", "z"))
+PAYLOAD_PARTS = (5, 3, 1)
+HIDDEN_ORDERS = (("x", "y"), ("y", "x"))
+HIDDEN_PARTS = (5, 3)
+TILE = 16
+
+
+def cut(rows, weights):
+    tiles = rows // TILE
+    sizes, done = [], 0
+    for i, w in enumerate(weights):
+        upto = tiles * sum(weights[: i + 1]) // sum(weights)
+        sizes.append((done * TILE, (upto - done) * TILE))
+        done = upto
+    return sizes
+
+
+def guarded(conditions, action):
+    live = [c for c in conditions if c is not None]
+    if not live:
+        action()
+        return
+    test = live[0]
+    for c in live[1:]:
+        test = jnp.logical_and(test, c)
+    pl.when(test)(action)
+
+
+class Gather:
+    def __init__(self, place, depth, view, orders, recv_sem, send_sem):
+        self.place, self.depth, self.view = place, depth, view
+        self.recv_sem, self.send_sem = recv_sem, send_sem
+        self.sends = []
+        found = []
+        for part, order in enumerate(orders):
+            reach = [(0, 0, 0, -1, 0)]
+            for step, dim in enumerate(order):
+                fresh = []
+                for rx, ry, dz, _, hops in reach:
+                    if dim == "x":
+                        fresh.append((1, ry, dz, step, hops + 1))
+                    elif dim == "y":
+                        fresh.append((rx, 1, dz, step, hops + 1))
+                    else:
+                        for k in range(1, depth):
+                            fresh.append((rx, ry, -k, step, hops + k))
+                            fresh.append((rx, ry, k, step, hops + k))
+                reach += fresh
+            found += [(hops, part, order, step, rx, ry, dz) for rx, ry, dz, step, hops in reach]
+        self.found = sorted(found, key=lambda f: f[0])
+        self.slot = {(f[1], f[4], f[5], f[6]): i for i, f in enumerate(self.found)}
+
+    @staticmethod
+    def counts(depth, orders):
+        pieces = sends = 0
+        for order in orders:
+            n = 1
+            for dim in order:
+                n *= 2 if dim in "xy" else 2 * depth - 1
+            pieces += n
+            sends += 3 * n
+        return pieces, sends
+
+    def exists(self, dz):
+        z = self.place[2]
+        if dz < 0:
+            return z + dz >= 0
+        if dz > 0:
+            return z + dz < self.depth
+        return None
+
+    def ref(self, part, rx, ry, dz):
+        x, y, z, _ = self.place
+        ox = 1 - x if rx else x
+        oy = 1 - y if ry else y
+        return self.view(part, ox, oy, z + dz)
+
+    def target(self, dim, sign):
+        x, y, z, c = self.place
+        if dim == "x":
+            x = 1 - x
+        elif dim == "y":
+            y = 1 - y
+        else:
+            z = z + sign
+        return ((z * 2 + y) * 2 + x, c)
+
+    def send(self, part, rx, ry, dz, dim, sign):
+        there = (part, rx ^ (dim == "x"), ry ^ (dim == "y"), dz - sign if dim == "z" else dz)
+        if there not in self.slot:
+            return
+        z = self.place[2]
+        conditions = [self.exists(dz)]
+        if dim == "z":
+            conditions.append(z + sign < self.depth if sign > 0 else z + sign >= 0)
+        block = self.ref(part, rx, ry, dz)
+        copy = pltpu.make_async_remote_copy(
+            src_ref=block,
+            dst_ref=block,
+            send_sem=self.send_sem.at[len(self.sends)],
+            recv_sem=self.recv_sem.at[self.slot[there]],
+            device_id=self.target(dim, sign),
+            device_id_type=MESH,
+        )
+        self.sends.append((conditions, copy))
+        guarded(conditions, copy.start)
+
+    def onward(self, entry):
+        _, part, order, step, rx, ry, dz = entry
+        if step >= 0 and order[step] == "z":
+            self.send(part, rx, ry, dz, "z", 1 if dz < 0 else -1)
+        for dim in order[step + 1 :]:
+            if dim == "z":
+                self.send(part, rx, ry, dz, "z", 1)
+                self.send(part, rx, ry, dz, "z", -1)
+            else:
+                self.send(part, rx, ry, dz, dim, 0)
+
+    def arrive(self, entry):
+        _, part, order, step, rx, ry, dz = entry
+        block = self.ref(part, rx, ry, dz)
+        copy = pltpu.make_async_remote_copy(
+            src_ref=block,
+            dst_ref=block,
+            send_sem=self.send_sem.at[0],
+            recv_sem=self.recv_sem.at[self.slot[(part, rx, ry, dz)]],
+            device_id=self.target("x", 0),
+            device_id_type=MESH,
+        )
+        guarded([self.exists(dz)], copy.wait_recv)
+
+    def own(self):
+        return [f for f in self.found if f[0] == 0]
+
+    def rest(self):
+        return [f for f in self.found if f[0] > 0]
+
+    def drain(self):
+        for conditions, copy in self.sends:
+            guarded(conditions, copy.wait_send)
+
+
+def exchange_kernel(
+    depth,
+    hidden_ref,
+    pack_ref,
+    cos_ref,
+    sin_ref,
+    kv_ref,
+    hid,
+    packs,
+    give,
+    full,
+    acc,
+    peer,
+    local_sem,
+    swap_sem,
+    peer_send,
+    peer_recv,
+    hid_recv,
+    hid_send,
+    w_recv,
+    w_send,
+    kv_recv,
+    kv_send,
+):
+    me = lax.axis_index("dp")
+    core = lax.axis_index("mp")
+    x = me % 2
+    y = (me // 2) % 2
+    z = me // 4
+    place = (x, y, z, core)
+    rows = hidden_ref.shape[0]
+    mine = y * 2 + x
+    across = (z * 4 + y * 2 + (1 - x), core)
+    along = (z * 4 + (1 - y) * 2 + x, core)
+    other = (me, 1 - core)
+
+    local = [
+        pltpu.make_async_copy(hidden_ref, hid.at[mine], local_sem.at[0]),
+        pltpu.make_async_copy(pack_ref.at[0], packs.at[z, x], local_sem.at[1]),
+        pltpu.make_async_copy(pack_ref.at[1], give, local_sem.at[2]),
+    ]
+    for copy in local:
+        copy.start()
+    barrier = pltpu.get_barrier_semaphore()
+
+    def greet(device):
+        pl.semaphore_signal(barrier, inc=1, device_id=device, device_id_type=MESH)
+
+    for device in (across, along, other):
+        greet(device)
+    pl.when(z > 0)(lambda: greet((me - 4, core)))
+    pl.when(z < depth - 1)(lambda: greet((me + 4, core)))
+    inner = jnp.logical_and(z > 0, z < depth - 1)
+    pl.when(inner)(lambda: pl.semaphore_wait(barrier, 5))
+    pl.when(jnp.logical_not(inner))(lambda: pl.semaphore_wait(barrier, 4 if depth > 1 else 3))
+    for copy in local:
+        copy.wait()
+
+    swap = pltpu.make_async_remote_copy(
+        src_ref=give,
+        dst_ref=packs.at[z, x],
+        send_sem=swap_sem.at[0],
+        recv_sem=swap_sem.at[1],
+        device_id=across,
+        device_id_type=MESH,
+    )
+    swap.start()
+
+    spans = cut(rows, HIDDEN_PARTS)
+
+    def hid_view(part, ox, oy, oz):
+        return hid.at[oy * 2 + ox, pl.ds(*spans[part])]
+
+    def w_view(part, ox, oy, oz):
+        half = x if part == 0 else 1 - x
+        return packs.at[oz, half]
+
+    hidden_gather = Gather(place, depth, hid_view, HIDDEN_ORDERS, hid_recv, hid_send)
+    w_gather = Gather(place, depth, w_view, (("z",), ("z",)), w_recv, w_send)
+    w_own = w_gather.own()
+    w_gather.onward(w_own[0])
+    for entry in hidden_gather.own():
+        hidden_gather.onward(entry)
+    swap.wait_recv()
+    w_gather.onward(w_own[1])
+    events = [(0.5 + f[0], 0, f) for f in w_gather.rest()]
+    events += [(1.0 * f[0], 1, f) for f in hidden_gather.rest()]
+    for _, which, entry in sorted(events, key=lambda e: e[0]):
+        gather = (w_gather, hidden_gather)[which]
+        gather.arrive(entry)
+        gather.onward(entry)
+
+    width = packs.shape[3] // 2
+    span = packs.shape[2]
+    for k in range(depth):
+        h0 = packs[k, 0]
+        h1 = packs[k, 1]
+        columns = pl.ds(k * 2 * width, 2 * width)
+        full[pl.ds(0, span), columns] = jnp.concatenate([h0[:, :width], h1[:, :width]], axis=1)
+        full[pl.ds(span, span), columns] = jnp.concatenate([h0[:, width:], h1[:, width:]], axis=1)
+
+    half_width = acc.shape[2]
+    sends = []
+    for i in range(4):
+        block = pl.ds(i * rows, rows)
+        for h in range(2):
+            acc[h, block] = jnp.dot(
+                hid[i],
+                full[:, pl.ds(h * half_width, half_width)],
+                preferred_element_type=jnp.float32,
+            )
+        copy = pltpu.make_async_remote_copy(
+            src_ref=acc.at[1 - core, block],
+            dst_ref=peer.at[block],
+            send_sem=peer_send.at[i],
+            recv_sem=peer_recv.at[i],
+            device_id=other,
+            device_id_type=MESH,
+        )
+        copy.start()
+        sends.append(copy)
+
+    heads = half_width // HD
+    for i in range(4):
+        sends[i].wait_recv()
+        block = pl.ds(i * rows, rows)
+        cosines = cos_ref[block]
+        sines = sin_ref[block]
+        for h in range(heads):
+            columns = pl.ds(h * HD, HD)
+            total = acc[core, block, columns] + peer[block, columns]
+            turned = total * cosines + pltpu.roll(total, HD // 2, 1) * sines
+            kv_ref[me, block, columns] = turned.astype(jnp.bfloat16)
+
+    kv_spans = cut(kv_ref.shape[1], PAYLOAD_PARTS)
+
+    def kv_view(part, ox, oy, oz):
+        return kv_ref.at[(oz * 2 + oy) * 2 + ox, pl.ds(*kv_spans[part])]
+
+    kv_gather = Gather(place, depth, kv_view, PAYLOAD_ORDERS, kv_recv, kv_send)
+    for entry in kv_gather.own():
+        kv_gather.onward(entry)
+    for entry in kv_gather.rest():
+        kv_gather.arrive(entry)
+        kv_gather.onward(entry)
+
+    swap.wait_send()
+    for copy in sends:
+        copy.wait_send()
+    hidden_gather.drain()
+    w_gather.drain()
+    kv_gather.drain()
+
+
+def attend_kernel(ratio, local_slots, tab_ref, q_ref, *refs):
+    blocks, out_ref = refs[:MAXB], refs[MAXB]
+    s = pl.program_id(0)
+    length = tab_ref[local_slots * MAXB + s]
+    start = tab_ref[local_slots * (MAXB + 1) + s] * BLOCK
+    keys = jnp.concatenate([b[0, 0, 0] for b in blocks], axis=0)
+    values = jnp.concatenate([b[0, 0, 1] for b in blocks], axis=0)
+    span = keys.shape[0]
+    row = start + lax.broadcasted_iota(jnp.int32, (BLOCK, span), 0)
+    col = lax.broadcasted_iota(jnp.int32, (BLOCK, span), 1)
+    allowed = (col <= row) & (col < length)
+    valid = (start + lax.broadcasted_iota(jnp.int32, (BLOCK, HD), 0)) < length
+    for r in range(ratio):
+        columns = pl.ds(r * HD, HD)
+        scores = lax.dot_general(
+            q_ref[:, columns], keys, (((1,), (1,)), ((), ())), preferred_element_type=jnp.float32
+        ) * (1.0 / math.sqrt(HD))
+        scores = jnp.where(allowed, scores, -1e30)
+        weights = jnp.exp(scores - jnp.max(scores, axis=1, keepdims=True))
+        probs = (weights / jnp.sum(weights, axis=1, keepdims=True)).astype(jnp.bfloat16)
+        mixed = jnp.dot(probs, values, preferred_element_type=jnp.float32)
+        out_ref[:, columns] = jnp.where(valid, mixed, 0.0).astype(jnp.bfloat16)
+
+
+def cache_kernel(local_heads, tab_ref, kv_ref, key_ref, value_ref):
+    m = pl.program_id(0)
+    length = tab_ref[MAXB]
+    place = m * BLOCK + lax.broadcasted_iota(jnp.int32, (BLOCK, HD), 0)
+    for g in range(local_heads):
+        columns = pl.ds(g * HD, HD)
+        inner = pl.ds(g // 2 * HD, HD)
+        for which, out in ((0, key_ref), (1, value_ref)):
+            block = kv_ref[0, g % 2, which, :, inner]
+            out[0, :, columns] = jnp.where(place < length, block, jnp.zeros_like(block))
+
+
+def fast_shards(hidden, w_key, w_value, queries, lengths, seq_of_slot, pos_of_slot):
+    replica = lax.axis_index("dp")
+    depth = lax.axis_size("dp") // 4
+    rows, features = hidden.shape
+    width = w_key.shape[1]
+    plane = 4 * rows
+    plane_slots = plane // BLOCK
+    half_width = depth * width
+    local_heads = 2 * half_width // HD
+    x = replica % 2
+    middle = features // 2
+    k_pack = jnp.concatenate([w_key[:middle], w_key[middle:]], axis=1)
+    v_pack = jnp.concatenate([w_value[:middle], w_value[middle:]], axis=1)
+    pack = jnp.stack([jnp.where(x == 0, k_pack, v_pack), jnp.where(x == 0, v_pack, k_pack)])
+
+    plane_pos = lax.dynamic_slice_in_dim(pos_of_slot, replica // 4 * plane_slots, plane_slots)
+    positions = (plane_pos[:, None] * BLOCK + jnp.arange(BLOCK, dtype=jnp.int32)[None, :]).reshape(plane)
+    lane = jnp.arange(HD, dtype=jnp.int32)
+    indices = (lane % (HD // 2)).astype(jnp.float32)
+    frequency = jnp.exp(-(2.0 * indices / HD) * math.log(500000.0))
+    angles = positions.astype(jnp.float32)[:, None] * frequency[None, :]
+    cosines = jnp.where(x == 0, jnp.cos(angles), 1.0)
+    sines = jnp.sin(angles)
+    sines = jnp.where(x == 0, jnp.where(lane[None, :] < HD // 2, -sines, sines), 0.0)
+
+    hid_counts = Gather.counts(depth, HIDDEN_ORDERS)
+    w_counts = Gather.counts(depth, (("z",), ("z",)))
+    kv_counts = Gather.counts(depth, PAYLOAD_ORDERS)
+    dma = pltpu.SemaphoreType.DMA
+    vmem = pl.BlockSpec(memory_space=pltpu.VMEM)
+    anywhere = pl.BlockSpec(memory_space=pl.ANY)
+    kv = pl.pallas_call(
+        functools.partial(exchange_kernel, depth),
+        out_shape=jax.ShapeDtypeStruct((4 * depth, plane, half_width), jnp.bfloat16),
+        in_specs=[anywhere, anywhere, vmem, vmem],
+        out_specs=vmem,
+        scratch_shapes=[
+            pltpu.VMEM((4, rows, features), jnp.bfloat16),
+            pltpu.VMEM((depth, 2, middle, 2 * width), jnp.bfloat16),
+            pltpu.VMEM((middle, 2 * width), jnp.bfloat16),
+            pltpu.VMEM((features, 2 * half_width), jnp.bfloat16),
+            pltpu.VMEM((2, plane, half_width), jnp.float32),
+            pltpu.VMEM((plane, half_width), jnp.float32),
+            dma((3,)),
+            dma((2,)),
+            dma((4,)),
+            dma((4,)),
+            dma((hid_counts[0],)),
+            dma((hid_counts[1],)),
+            dma((w_counts[0],)),
+            dma((w_counts[1],)),
+            dma((kv_counts[0],)),
+            dma((kv_counts[1],)),
+        ],
+        compiler_params=pltpu.CompilerParams(
+            collective_id=0, has_side_effects=True, vmem_limit_bytes=60 * 2**20
+        ),
+    )(hidden, pack, cosines, sines)
+    kv = kv.reshape(depth, 2, 2, plane, half_width)
+
+    slots = rows // BLOCK
+    my_seq = lax.dynamic_slice_in_dim(seq_of_slot, replica * slots, slots)
+    my_pos = lax.dynamic_slice_in_dim(pos_of_slot, replica * slots, slots)
+    wanted = jnp.concatenate([my_seq, replica[None].astype(jnp.int32)])
+    blocks = jnp.arange(MAXB, dtype=jnp.int32)
+    ids = jnp.arange(seq_of_slot.shape[0], dtype=jnp.int32)
+    match = (seq_of_slot[None, None, :] == wanted[:, None, None]) & (
+        pos_of_slot[None, None, :] == blocks[None, :, None]
+    )
+    source = jnp.sum(jnp.where(match, ids[None, None, :], 0), axis=2)
+    bounds = jnp.sum(jnp.where(wanted[:, None] == jnp.arange(lengths.shape[0])[None, :], lengths[None, :], 0), axis=1)
+    table = jnp.concatenate([source[:slots].reshape(-1), bounds[:slots], my_pos]).astype(jnp.int32)
+    home = jnp.concatenate([source[slots], bounds[slots:]]).astype(jnp.int32)
+
+    def block_spec(m):
+        def index(s, g, tab):
+            slot = tab[s * MAXB + m]
+            return (slot // plane_slots, g % 2, 0, slot % plane_slots, g // 2)
+
+        return pl.BlockSpec((1, 1, 2, BLOCK, HD), index)
+
+    group = queries.shape[1] // local_heads
+    context = pl.pallas_call(
+        functools.partial(attend_kernel, group // HD, slots),
+        out_shape=jax.ShapeDtypeStruct(queries.shape, jnp.bfloat16),
+        grid_spec=pltpu.PrefetchScalarGridSpec(
+            num_scalar_prefetch=1,
+            grid=(slots, local_heads),
+            in_specs=[pl.BlockSpec((BLOCK, group), lambda s, g, tab: (s, g))]
+            + [block_spec(m) for m in range(MAXB)],
+            out_specs=pl.BlockSpec((BLOCK, group), lambda s, g, tab: (s, g)),
+        ),
+    )(table, queries, *([kv] * MAXB))
+
+    cache = jax.ShapeDtypeStruct((1, MAXB * BLOCK, local_heads * HD), jnp.bfloat16)
+    cache_spec = pl.BlockSpec((1, BLOCK, local_heads * HD), lambda m, tab: (0, m, 0))
+    key_cache, value_cache = pl.pallas_call(
+        functools.partial(cache_kernel, local_heads),
+        out_shape=(cache, cache),
+        grid_spec=pltpu.PrefetchScalarGridSpec(
+            num_scalar_prefetch=1,
+            grid=(MAXB,),
+            in_specs=[
+                pl.BlockSpec(
+                    (1, 2, 2, BLOCK, half_width),
+                    lambda m, tab: (tab[m] // plane_slots, 0, 0, tab[m] % plane_slots, 0),
+                )
+            ],
+            out_specs=(cache_spec, cache_spec),
+        ),
+    )(home, kv)
+    return context, key_cache, value_cache
+
+
+def suits(mesh):
+    replicas, halves = mesh.shape["dp"], mesh.shape["mp"]
+    return halves == 2 and replicas % 8 == 0 and KVH * HD == replicas * (HD // 2)
+
+
 def solution(mesh):
     in_specs = (P("dp", "mp"), P("mp", "dp"), P("mp", "dp"), P("dp", "mp"), P(), P(), P())
     out_specs = (P("dp", "mp"), P("dp", None, "mp"), P("dp", None, "mp"))
-    return jax.shard_map(shards, mesh=mesh, in_specs=in_specs, out_specs=out_specs, check_vma=False)
+    return jax.shard_map(fast_shards if suits(mesh) else shards, mesh=mesh, in_specs=in_specs, out_specs=out_specs, check_vma=False)

time: 452 us -> 233 us (0.52)
  waiting for transfers between devices: 344 us -> 0 us
  Pallas kernels: 0 us -> 218 us
  matrix products: 43.9 us -> 0 us
  local copies, waits for them, and re-layouts: 43.5 us -> 4.34 us
  between operations: 14 us -> 0.74 us
    all_gather x3 -> x0, waiting for transfers between devices: 331 us -> none  [the longest x1 117 us: shards(): lax.all_gather(w_key, 'dp', axis=1, tiled=True)]
    pallas_call x0 -> x3, Pallas kernels: none -> 218 us  [the longest x1 186 us: fast_shards(): pl.pallas_call(functools.partial(exchange_kernel, depth), out_shape=jax.S...]
    dot_general x5 -> x0, matrix products: 33.3 us -> none  [the longest x1 8.68 us: shards(): jnp.einsum('sgrbc,scgd->sbgrd', probs, value_blocks, preferred_element_ty...]
    unnamed x18 -> x6, local copies, waits for them, and re-layouts: 23 us -> 1.11 us
    reduce_scatter x2 -> x0, waiting for transfers between devices: 11.4 us -> none  [the longest x1 10.1 us: shards(): lax.psum_scatter(value_sum, 'mp', scatter_dimension=1, tiled=True)]
    sub x1 -> x0, matrix products: 10.7 us -> none  [shards(): weights = jnp.exp(scores - largest)]
    convert_element_type x3 -> x0, local copies, waits for them, and re-layouts: 9.59 us -> none  [the longest x2 8.7 us: shards(): mixed.reshape(token_rows, local_heads * ratio * HD).astype(jnp.bfloat16)]
    reshape x3 -> x1, local copies, waits for them, and re-layouts: 6.17 us -> 0.08 us  [fast_shards(): source[:slots].reshape(-1)]
  transfers between devices with their start and end apart: 5 -> 0, of which waited for: 5 -> 0; matrix products, arithmetic and copies ran while one was open for 5% -> 0% of each run, Pallas kernels for 0% -> 0%
where the time goes in v1:
time: 233 us
  Pallas kernels  218 us (94%)
  other arithmetic  9.95 us (4%)
  local copies, waits for them, and re-layouts  4.34 us (2%)
    pallas_call x1, Pallas kernels, fast_shards(): pl.pallas_call(functools.partial(exchange_kernel, depth), out_shape=jax.S...  186 us
    pallas_call x1, Pallas kernels, fast_shards(): pl.pallas_call(functools.partial(attend_kernel, group // HD, slots), out_...  27.4 us

profile of v1, /device:TPU:0, one launch (start us, length us, event | category | flops | bytes accessed | tf_op | source)
XLA Modules:
  0.0 232.8 jit_solution(9171378929268223906)
XLA Ops:
  0.6 0.0 copy-start
  0.7 0.8 dynamic-slice_multiply_fusion
  1.5 0.7 dynamic_slice.9
  2.2 0.1 pad_add_fusion
  2.3 0.7 dynamic_slice.10
  3.0 0.8 select_reduce_fusion.1
  3.8 0.6 slice.31
  4.4 0.7 broadcast_compare_fusion
  5.1 0.7 iota_compare_fusion.1
  5.8 0.2 select_reduce_fusion
  6.0 0.1 reshape.213
  6.1 0.6 pad_add_fusion.1.tab_ref
  6.7 1.2 pad_add_fusion.2.tab_ref
  7.9 0.1 convert_bitcast_fusion
  8.0 1.1 fusion.7
  9.0 0.3 copy.18
  9.3 0.3 copy.19
  9.6 0.0 copy-done
  9.7 0.3 copy.20
  9.9 0.3 copy.21
  10.2 0.6 broadcast_select_fusion.1
  10.9 1.1 pad_maximum_fusion.pack_ref
  11.9 3.1 %fusion.1 = (f32[1024,128]{1,0:T(8,128)}, f32[1024,128]{1,0:T(8,128)}) fusion(f32[128]{0:T(128)S(1)} %fusion.6, f32[1024]{0:T(1024)S(1)} %convert_bitcast_fusion, pred[128]{0:T(512)(128)(4,1)S(1)} %iota_compare_fusion.2, pred[]{:T(512)S(6)} %eq.68), kind=kLoop, calls=%fused_computation.5 | loop fusion | flops 655360 | bytes 1053313 | tf_op jit(solution)/shard_map/jit(_where)/select_n | solution.py:461
  15.0 186.3 %shard_map.94 = bf16[16,1024,256]{2,1,0:T(8,128)(2,1)} custom-call(bf16[256,4096]{1,0:T(8,128)(2,1)} %hidden_ref.1, bf16[2,2048,128]{2,1,0:T(8,128)(2,1)} %pad_maximum_fusion.pack_ref, f32[1024,128]{1,0:T(8,128)} %get-tuple-element.14.cos_ref, f32[1024,128]{1,0:T(8,128)} %get-tuple-element.13.sin_ref), custom_call_target="tpu_custom_call" | custom-call | tf_op jit(solution)/shard_map/pallas_call | solution.py:469
  201.3 4.1 %shard_map.96 = (bf16[1,512,512]{2,1,0:T(8,128)(2,1)}, bf16[1,512,512]{2,1,0:T(8,128)(2,1)}) custom-call(s32[5]{0:T(128)} %pad_add_fusion.2.tab_ref, bf16[4,2,2,1024,256]{4,3,2,1,0:T(8,128)(2,1)} %bitcast.11), custom_call_target="tpu_custom_call" | custom-call | tf_op jit(solution)/shard_map/pallas_call | solution.py:534
  205.4 27.4 %shard_map.95 = bf16[256,4096]{1,0:T(8,128)(2,1)} custom-call(s32[12]{0:T(128)} %pad_add_fusion.1.tab_ref, bf16[256,4096]{1,0:T(8,128)(2,1)} %q_ref.1, bf16[4,2,2,1024,256]{4,3,2,1,0:T(8,128)(2,1)} %bitcast.12, bf16[4,2,2,1024,256]{4,3,2,1,0:T(8,128)(2,1)} %bitcast.13, bf16[4,2,2,1024,256]{4,3,2,1,0:T(8,128)(2,1)} %bitcast.14, ...), custom_call_target="tpu_custom_call" | custom-call | tf_op jit(solution)/shard_map/pallas_call | solution.py:520
  (5 shorter events, 0.1 us)
Async XLA Ops:
  0.6 9.0 %copy-start = (bf16[4096,64]{0,1:T(8,128)(2,1)S(1)}, bf16[4096,64]{0,1:T(8,128)(2,1)}, u32[]{:S(2)}) copy-start(bf16[4096,64]{0,1:T(8,128)(2,1)} %param.9) | copy-start | bytes 1572868

commit v2 on v1

--- a/solution.py
+++ b/solution.py
@@ -108,6 +108,7 @@
 HIDDEN_ORDERS = (("x", "y"), ("y", "x"))
 HIDDEN_PARTS = (5, 3)
 TILE = 16
+PAIR = 2
 
 
 def cut(rows, weights):
@@ -152,8 +153,13 @@
                             fresh.append((rx, ry, k, step, hops + k))
                 reach += fresh
             found += [(hops, part, order, step, rx, ry, dz) for rx, ry, dz, step, hops in reach]
-        self.found = sorted(found, key=lambda f: f[0])
+        self.found = sorted(found, key=lambda f: (self.final(f), f[0], f[3] - len(f[2])))
         self.slot = {(f[1], f[4], f[5], f[6]): i for i, f in enumerate(self.found)}
+
+    @staticmethod
+    def final(entry):
+        _, _, order, step, _, _, _ = entry
+        return step == len(order) - 1 and order[step] != "z"
 
     @staticmethod
     def counts(depth, orders):
@@ -330,8 +336,10 @@
         hidden_gather.onward(entry)
     swap.wait_recv()
     w_gather.onward(w_own[1])
-    events = [(0.5 + f[0], 0, f) for f in w_gather.rest()]
-    events += [(1.0 * f[0], 1, f) for f in hidden_gather.rest()]
+    events = [(2.0 * f[0] - 1 + f[1], 0, f) for f in w_gather.rest()]
+    events += [
+        (100.0 if Gather.final(f) else 3.5 + 0.7 * f[1], 1, f) for f in hidden_gather.rest()
+    ]
     for _, which, entry in sorted(events, key=lambda e: e[0]):
         gather = (w_gather, hidden_gather)[which]
         gather.arrive(entry)
@@ -409,18 +417,23 @@
     span = keys.shape[0]
     row = start + lax.broadcasted_iota(jnp.int32, (BLOCK, span), 0)
     col = lax.broadcasted_iota(jnp.int32, (BLOCK, span), 1)
-    allowed = (col <= row) & (col < length)
+    bias = jnp.where((col <= row) & (col < length), 0.0, -1e30)
+    bias = jnp.concatenate([bias] * PAIR, axis=0)
     valid = (start + lax.broadcasted_iota(jnp.int32, (BLOCK, HD), 0)) < length
-    for r in range(ratio):
-        columns = pl.ds(r * HD, HD)
+    for r in range(0, ratio, PAIR):
+        q = jnp.concatenate([q_ref[:, pl.ds((r + i) * HD, HD)] for i in range(PAIR)], axis=0)
         scores = lax.dot_general(
-            q_ref[:, columns], keys, (((1,), (1,)), ((), ())), preferred_element_type=jnp.float32
-        ) * (1.0 / math.sqrt(HD))
-        scores = jnp.where(allowed, scores, -1e30)
-        weights = jnp.exp(scores - jnp.max(scores, axis=1, keepdims=True))
-        probs = (weights / jnp.sum(weights, axis=1, keepdims=True)).astype(jnp.bfloat16)
-        mixed = jnp.dot(probs, values, preferred_element_type=jnp.float32)
-        out_ref[:, columns] = jnp.where(valid, mixed, 0.0).astype(jnp.bfloat16)
+            q, keys, (((1,), (1,)), ((), ())), preferred_element_type=jnp.float32
+        )
+        scores = scores + bias
+        largest = jnp.max(scores, axis=1, keepdims=True)
+        weights = jnp.exp2((scores - largest) * (math.log2(math.e) / math.sqrt(HD)))
+        scale = 1.0 / jnp.sum(weights, axis=1, keepdims=True)
+        mixed = jnp.dot(weights.astype(jnp.bfloat16), values, preferred_element_type=jnp.float32)
+        mixed = mixed * scale
+        for i in range(PAIR):
+            part = jnp.where(valid, mixed[i * BLOCK : (i + 1) * BLOCK], 0.0)
+            out_ref[:, pl.ds((r + i) * HD, HD)] = part.astype(jnp.bfloat16)
 
 
 def cache_kernel(local_heads, tab_ref, kv_ref, key_ref, value_ref):

time: 233 us -> 188 us (0.81)
  Pallas kernels: 218 us -> 173 us
    pallas_call x1, Pallas kernels: 186 us -> 154 us  [fast_shards(): pl.pallas_call(functools.partial(exchange_kernel, depth), out_shape=jax.S...]
    pallas_call x1, Pallas kernels: 27.4 us -> 15.1 us  [fast_shards(): pl.pallas_call(functools.partial(attend_kernel, group // HD, slots), out_...]
where the time goes in v2:
time: 188 us
  Pallas kernels  173 us (92%)
  other arithmetic  9.95 us (5%)
  local copies, waits for them, and re-layouts  4.34 us (2%)
    pallas_call x1, Pallas kernels, fast_shards(): pl.pallas_call(functools.partial(exchange_kernel, depth), out_shape=jax.S...  154 us
    pallas_call x1, Pallas kernels, fast_shards(): pl.pallas_call(functools.partial(attend_kernel, group // HD, slots), out_...  15.1 us

profile of v2, /device:TPU:0, one launch (start us, length us, event | category | flops | bytes accessed | tf_op | source)
XLA Modules:
  0.0 187.9 jit_solution(14575431114589422599)
XLA Ops:
  0.6 0.0 copy-start
  0.7 0.8 dynamic-slice_multiply_fusion
  1.5 0.7 dynamic_slice.9
  2.2 0.1 pad_add_fusion
  2.3 0.7 dynamic_slice.10
  3.0 0.8 select_reduce_fusion.1
  3.8 0.6 slice.31
  4.4 0.7 broadcast_compare_fusion
  5.1 0.7 iota_compare_fusion.1
  5.8 0.2 select_reduce_fusion
  6.0 0.1 reshape.213
  6.1 0.6 pad_add_fusion.1.tab_ref
  6.7 1.2 pad_add_fusion.2.tab_ref
  7.9 0.1 convert_bitcast_fusion
  8.0 1.1 fusion.7
  9.0 0.3 copy.18
  9.3 0.3 copy.19
  9.6 0.0 copy-done
  9.7 0.3 copy.20
  9.9 0.3 copy.21
  10.2 0.6 broadcast_select_fusion.1
  10.9 1.1 pad_maximum_fusion.pack_ref
  11.9 3.1 %fusion.1 = (f32[1024,128]{1,0:T(8,128)}, f32[1024,128]{1,0:T(8,128)}) fusion(f32[128]{0:T(128)S(1)} %fusion.6, f32[1024]{0:T(1024)S(1)} %convert_bitcast_fusion, pred[128]{0:T(512)(128)(4,1)S(1)} %iota_compare_fusion.2, pred[]{:T(512)S(6)} %eq.68), kind=kLoop, calls=%fused_computation.5 | loop fusion | flops 655360 | bytes 1053313 | tf_op jit(solution)/shard_map/jit(_where)/select_n | solution.py:474
  15.0 154.0 %shard_map.94 = bf16[16,1024,256]{2,1,0:T(8,128)(2,1)} custom-call(bf16[256,4096]{1,0:T(8,128)(2,1)} %hidden_ref.1, bf16[2,2048,128]{2,1,0:T(8,128)(2,1)} %pad_maximum_fusion.pack_ref, f32[1024,128]{1,0:T(8,128)} %get-tuple-element.14.cos_ref, f32[1024,128]{1,0:T(8,128)} %get-tuple-element.13.sin_ref), custom_call_target="tpu_custom_call" | custom-call | tf_op jit(solution)/shard_map/pallas_call | solution.py:482
  169.1 3.7 %shard_map.96 = (bf16[1,512,512]{2,1,0:T(8,128)(2,1)}, bf16[1,512,512]{2,1,0:T(8,128)(2,1)}) custom-call(s32[5]{0:T(128)} %pad_add_fusion.2.tab_ref, bf16[4,2,2,1024,256]{4,3,2,1,0:T(8,128)(2,1)} %bitcast.11), custom_call_target="tpu_custom_call" | custom-call | tf_op jit(solution)/shard_map/pallas_call | solution.py:547
  172.8 15.1 %shard_map.95 = bf16[256,4096]{1,0:T(8,128)(2,1)} custom-call(s32[12]{0:T(128)} %pad_add_fusion.1.tab_ref, bf16[256,4096]{1,0:T(8,128)(2,1)} %q_ref.1, bf16[4,2,2,1024,256]{4,3,2,1,0:T(8,128)(2,1)} %bitcast.12, bf16[4,2,2,1024,256]{4,3,2,1,0:T(8,128)(2,1)} %bitcast.13, bf16[4,2,2,1024,256]{4,3,2,1,0:T(8,128)(2,1)} %bitcast.14, ...), custom_call_target="tpu_custom_call" | custom-call | tf_op jit(solution)/shard_map/pallas_call | solution.py:533
  (5 shorter events, 0.1 us)
Async XLA Ops:
  0.6 9.0 %copy-start = (bf16[4096,64]{0,1:T(8,128)(2,1)S(1)}, bf16[4096,64]{0,1:T(8,128)(2,1)}, u32[]{:S(2)}) copy-start(bf16[4096,64]{0,1:T(8,128)(2,1)} %param.9) | copy-start | bytes 1572868
